TPU v7x, 32 devices: a whole 2x2x4 slice. The times are simulated.
32 devices in a mesh: group: 2 (over x), tile: 16 (over z, y, core).
Axes of the slice: x: 2, y: 2, z: 4, core: 2. Of those that a mesh axis runs over, the one named last changes fastest.
Arguments:
- latents: bfloat16 [384, 16, 128], P(('group', 'tile')), parts along dimension 0, may hold values from -6 to 6
- clip_index: int32 [8], P('group'), parts along dimension 0, may hold values from 0 to 1, never falling along the last dimension, each value on 1 to 3 neighbouring positions
- first_conv: bfloat16 [3, 3, 3, 16, 384], replicated, may hold values from -0.3125 to 0.3125
- first_gain: float32 [384], replicated, may hold values from 0.4 to 1.6
- middle_conv: bfloat16 [3, 3, 3, 384, 384], replicated, may hold values from -0.0625 to 0.0625
- head_gain: float32 [384], replicated, may hold values from 0.4 to 1.6
- head_weight: bfloat16 [384, 48], replicated, may hold values from -0.3125 to 0.3125
Outputs:
- pixels: float32 [32, 2, 3, 48, 128], P(('group', 'tile')), parts along dimension 0
There are 2 independent parts, one for each index of `group`. A program takes and returns all parts, laid end to end along the dimension named above; an argument that names none is the same for every part. Nothing has to cross between parts.
Inputs may be any that keep to these rules, and one draw needn't show every extreme that they name: `clip_index`: clip numbers never fall along the frames; each clip holds 1 to 3 consecutive frames.
All inputs are finite; a program needn't handle non-finite values.
Results may differ from a plain program's by a relative error of at most 0.01.
Values may be sent and summed in bfloat16 or wider, within the bound.
No kernel may reach another device: no remote copies, remote signals or barrier semaphores. Data moves between devices by JAX's collectives and lax.ppermute only.
A program may use at most 128 MiB of HBM per device.

v0:
```python
import functools

import jax
import jax.numpy as jnp
from jax import lax
from jax.experimental import pallas as pl
from jax.experimental.pallas import tpu as pltpu
from jax.sharding import PartitionSpec as P

CLAT = 16
CH = 384
PATCH = 16
STRIPS = 8
TF = 2
WS = 16
HL = 48
LANE = 128
PER_TILE = LANE // CLAT
TILES_WIN = 3
SKIP = (PER_TILE - 3) * CLAT
PAIRS = 10
COLS = 2 * PAIRS
OUT_COLS = WS + 1
CELLS = PAIRS * HL
OUT_HALF = OUT_COLS * HL // 2
PAD = 8
STEP = 64
LT = CH // LANE


def silu_of_twice(half):
    return half + half * jnp.tanh(half)


def inv_rms(x):
    return lax.rsqrt(jnp.mean(x * x, axis=-1, keepdims=True) + 1e-06)


def position(place_ref, tiles):
    rotated = lax.rem(place_ref[0] - (STRIPS // 2 - 1) + tiles, tiles)
    return lax.rem(rotated, STRIPS), lax.div(rotated, STRIPS)


def frame_ids(clip_ref, block):
    ids = []
    for slot in range(6):
        frame = block * TF - 4 + slot
        known = clip_ref[jnp.maximum(frame, 0)]
        ids.append(jnp.where(frame >= 0, known, -1))
    return ids


def flag(condition):
    return jnp.where(condition, 1.0, 0.0).astype(jnp.float32)


def weights_kernel(tiles, place_ref, clip_ref, mc_ref, fc_ref, out_ref, b1_ref, gbuf, mbuf, insem, outsem):
    f32, bf16 = jnp.float32, jnp.bfloat16
    loads = []
    for dr in range(3):
        load = pltpu.make_async_copy(mc_ref.at[:, dr], gbuf.at[:, dr], insem.at[dr])
        load.start()
        loads.append(load)
    _, block = position(place_ref, tiles)
    ids = frame_ids(clip_ref, block)
    same = flag(ids[4] == ids[5])
    scale = 1.0 - 0.5 * same

    b1_ref[...] = jnp.zeros_like(b1_ref)
    for dt in range(3):
        for dr in range(3):
            for dc in range(3):
                at = dr * 64 + dc * CLAT
                taps = fc_ref[dt, dr, dc]
                b1_ref[dt, at : at + CLAT, :CH] = taps
                b1_ref[dt, at + CLAT : at + 2 * CLAT, CH:] = taps

    stores = []
    for dr in range(3):
        loads[dr].wait()
        for dc in range(3):
            tap = dr * 3 + dc

            def rows(i, carry):
                at = pl.multiple_of(i * STEP, STEP)
                g0, g1, g2 = (gbuf[dt, dr, dc, pl.ds(at, STEP), :].astype(f32) for dt in range(3))
                s0 = same * g0
                mbuf[tap, 0, pl.ds(at, STEP), :] = (scale * (g1 + (s0 + same * g2))).astype(bf16)
                mbuf[tap, 1, pl.ds(at, STEP), :] = (scale * (g2 + (s0 - same * g1))).astype(bf16)
                return carry

            lax.fori_loop(0, CH // STEP, rows, 0)
            for m in range(2):
                store = pltpu.make_async_copy(
                    mbuf.at[tap, m], out_ref.at[m, pl.ds(tap * CH, CH)], outsem.at[tap * 2 + m]
                )
                store.start()
                stores.append(store)
    for store in stores:
        store.wait()


def decode_kernel(
    slots,
    place_ref,
    clip_ref,
    recv_ref,
    b1_ref,
    fg_ref,
    wt_ref,
    mc_ref,
    hg_ref,
    hw_ref,
    out_ref,
    wbuf,
    hbuf,
    hwbuf,
    vf,
    x1,
    act,
    first,
    xa,
    ysum,
    wsem,
):
    f32, bf16 = jnp.float32, jnp.bfloat16
    copies = []
    for m in range(4):
        group = []
        for dr in range(3):
            for dc in range(3):
                tap = pl.ds((dr * 3 + dc) * CH, CH)
                source = mc_ref.at[m // 3 * 2, dr, dc] if m in (0, 3) else wt_ref.at[m - 1, tap]
                copy = pltpu.make_async_copy(source, wbuf.at[m, tap], wsem.at[m * 9 + dr * 3 + dc])
                copy.start()
                group.append(copy)
        copies.append(group)

    column, block = position(place_ref, recv_ref.shape[0])
    ids = frame_ids(clip_ref, block)
    inner_left = flag(column > 0)
    inner_right = flag(column < STRIPS - 1)
    hwbuf[...] = jnp.zeros_like(hwbuf)
    hwbuf[: 3 * PATCH] = hw_ref[...]

    vf[...] = jnp.zeros_like(vf)
    for slot in range(6 - slots, 6):
        base = jnp.maximum(block * TF - 4 + slot, 0) * 4
        for quarter in range(4):
            for tile in range(TILES_WIN):
                vf[PAD + 12 * quarter : PAD + 12 * quarter + 12, tile * LANE : (tile + 1) * LANE] = (
                    recv_ref[base + quarter, 12 * tile : 12 * tile + 12].astype(f32)
                )
        rows = [vf[PAD - 1 + dr : PAD - 1 + dr + HL, :] for dr in range(3)]
        for pair in range(PAIRS):
            at = 32 * pair
            x1[slot - 6 + slots, pair * HL : (pair + 1) * HL, :] = jnp.concatenate(
                [row[:, at : at + 64] for row in rows], axis=-1
            ).astype(bf16)

    for t in range(4):
        for col in range(COLS):
            for lt in range(LT):
                act[t, col, lt, 0:PAD, :] = jnp.zeros((PAD, LANE), f32)
                act[t, col, lt, PAD + HL :, :] = jnp.zeros((PAD, LANE), f32)
    gain = 0.5 * fg_ref[...].reshape(1, CH)
    same = flag(ids[4] == ids[5])
    keeps = [flag(ids[2] == ids[4]), flag(ids[3] == ids[4]), None, None]
    for t in range(4):
        total = None
        for dt in range(3):
            slot = t + dt
            if slot < 6 - slots:
                continue
            left = x1[slot - 6 + slots]
            if dt < 2:
                left = left * flag(ids[slot] == ids[t + 2]).astype(bf16)
            part = jnp.dot(left, b1_ref[dt], preferred_element_type=f32)
            total = part if total is None else total + part
        for side in range(2):
            x = total[:, side * CH : (side + 1) * CH]
            a = silu_of_twice(x * inv_rms(x) * gain)
            if keeps[t] is not None:
                a = a * keeps[t]
            for pair in range(PAIRS):
                cut = slice(pair * HL, (pair + 1) * HL)
                piece = a[cut]
                if pair == 0:
                    piece = piece * inner_left
                if pair == PAIRS - 1:
                    piece = piece * inner_right
                for lt in range(LT):
                    lanes = slice(lt * LANE, (lt + 1) * LANE)
                    act[t, 2 * pair + side, lt, PAD : PAD + HL, :] = piece[:, lanes]
                    if t >= 2:
                        first[t - 2, 2 * pair + side, lt] = x[cut, lanes]

    def transform(pair, carry):
        at = pl.multiple_of(pair * HL, HL)
        for lt in range(LT):
            sides = []
            for side in range(2):
                timed = []
                for k in range(4):
                    d = [act[t, 2 * pair + side, lt, pl.ds(PAD - 1 + k, HL // 2, stride=2), :] for t in range(4)]
                    s1, s2 = same * d[1], same * d[2]
                    timed.append((d[0] - s2, d[1] + s2, d[2] - s1, d[3] - s1))
                mixed = []
                for m in range(4):
                    r0, r1, r2, r3 = (timed[k][m] for k in range(4))
                    mixed += [r0 - r2, r1 + r2, r2 - r1, r1 - r3]
                sides.append(mixed)
            for k in range(16):
                both = jnp.concatenate([sides[0][k], sides[1][k]], axis=0).astype(bf16)
                xa[k, pl.ds(at, HL), lt * LANE : (lt + 1) * LANE] = both
        return carry

    lax.fori_loop(0, PAIRS, transform, 0, unroll=2)

    deep = 3 * CH
    for m in range(4):
        for copy in copies[m]:
            copy.wait()
        low, mid, high = (wbuf[m, dr * deep : (dr + 1) * deep, :] for dr in range(3))
        outer = low + high
        hbuf[m, :deep, :] = outer + mid
        hbuf[m, deep:, :] = outer - mid
        parts = []
        for n in range(4):
            k = 4 * m + n
            left = jnp.concatenate(
                [xa[k, 0:OUT_HALF, :], xa[k, HL // 2 : HL // 2 + OUT_HALF, :], xa[k, HL : HL + OUT_HALF, :]], axis=-1
            )
            right = hbuf[m, (n - 1) * deep : n * deep, :] if n in (1, 2) else wbuf[m, n // 3 * 2 * deep : (n // 3 * 2 + 1) * deep, :]
            parts.append(jnp.dot(left, right, preferred_element_type=f32))
        middle = (
            parts[0] + 0.5 * (parts[1] + parts[2]),
            0.5 * (parts[1] - parts[2]) - parts[3],
        )
        for p in range(2):
            if m == 0:
                ysum[0, p] = middle[p]
            elif m == 1:
                ysum[0, p] += middle[p]
                ysum[1, p] = same * middle[p]
            elif m == 2:
                ysum[0, p] += middle[p]
                ysum[1, p] -= same * middle[p]
            else:
                ysum[1, p] += middle[p]

    hgain = 0.5 * hg_ref[...].reshape(1, CH)
    lane = lax.broadcasted_iota(jnp.int32, (HL // 2, LANE), 1)
    for t in range(2):
        for p in range(2):
            rest = jnp.concatenate(
                [
                    jnp.concatenate(
                        [first[t, col, lt, pl.ds(p, HL // 2, stride=2), :] for lt in range(LT)], axis=-1
                    )
                    for col in range(1, 1 + OUT_COLS)
                ],
                axis=0,
            )
            x = ysum[t, p] + rest
            outward = silu_of_twice(x * inv_rms(x) * hgain).astype(bf16)
            patch = lax.dot_general(outward, hwbuf[...], (((1,), (1,)), ((), ())), preferred_element_type=f32)
            for colour in range(3):
                sums = [jnp.zeros((HL // 2, LANE), f32), jnp.zeros((HL // 2, LANE), f32)]
                for w in range(-1, WS):
                    cell = patch[(w + 1) * HL // 2 : (w + 2) * HL // 2]
                    if w < 0:
                        cell = cell * inner_left
                    turned = pltpu.roll(cell, (8 * w - PATCH * colour) % LANE, 1)
                    inside = (lane >= 8 * w) & (lane < 8 * w + PATCH)
                    sums[w % 2] = jnp.where(inside, turned, sums[w % 2])
                out_ref[0, t, colour, pl.ds(p, HL // 2, stride=2), :] = sums[0] + sums[1]


def window_kernel(tiles, latents_ref, out_ref, columns, packed_ref, moved):
    count, rows = packed_ref.shape[0], packed_ref.shape[1]
    flat = latents_ref[...].astype(jnp.float32).reshape(rows * CLAT, count * PER_TILE)
    for at in range(0, rows * CLAT, LANE):
        wide = min(LANE, rows * CLAT - at)
        columns[at // LANE, :, :wide] = flat[at : at + wide].T
    lane = lax.broadcasted_iota(jnp.int32, (count, LANE), 1)
    for row in range(rows):
        at = row * CLAT
        total = jnp.zeros((count, LANE), jnp.float32)
        for within in range(PER_TILE):
            piece = columns[at // LANE, pl.ds(within, count, stride=PER_TILE), :]
            piece = pltpu.roll(piece, (within * CLAT - at) % LANE, 1)
            total = jnp.where((lane >= within * CLAT) & (lane < (within + 1) * CLAT), piece, total)
        packed_ref[:, row, :] = total
    lane = lax.broadcasted_iota(jnp.int32, (rows, LANE), 1)
    turned = [jnp.zeros((rows, LANE), jnp.float32)]
    for tile in range(count):
        turned.append(pltpu.roll(packed_ref[tile], LANE - SKIP, 1))
    turned.append(jnp.zeros((rows, LANE), jnp.float32))
    for tile in range(count + 1):
        moved[tile] = jnp.where(lane < LANE - SKIP, turned[tile], turned[tile + 1]).astype(out_ref.dtype)
    for dest in range(tiles):
        strip = (dest - (STRIPS // 2 - 1)) % tiles % STRIPS
        for tile in range(TILES_WIN):
            if 2 * strip + tile <= count:
                out_ref[dest, tile * rows : (tile + 1) * rows] = moved[2 * strip + tile]
            else:
                out_ref[dest, tile * rows : (tile + 1) * rows] = jnp.zeros((rows, LANE), out_ref.dtype)


def per_device(latents, clip_index, first_conv, first_gain, middle_conv, head_gain, head_weight):
    tiles = lax.axis_size("tile")
    place = lax.axis_index("tile").astype(jnp.int32).reshape(1)
    rows = latents.shape[0]
    width = latents.shape[2]
    blocks = tiles // STRIPS
    slots = min(6, blocks * TF)
    sent = pl.pallas_call(
        functools.partial(window_kernel, tiles),
        out_shape=jax.ShapeDtypeStruct((tiles, TILES_WIN * rows, LANE), latents.dtype),
        in_specs=[pl.BlockSpec(memory_space=pltpu.VMEM)],
        out_specs=pl.BlockSpec(memory_space=pltpu.VMEM),
        scratch_shapes=[
            pltpu.VMEM((pl.cdiv(rows * CLAT, LANE), width, LANE), jnp.float32),
            pltpu.VMEM((width // PER_TILE, rows, LANE), jnp.float32),
            pltpu.VMEM((width // PER_TILE + 1, rows, LANE), latents.dtype),
        ],
        compiler_params=pltpu.CompilerParams(vmem_limit_bytes=8 * 1024 * 1024),
    )(latents)
    came = lax.all_to_all(sent, "tile", 0, 0, tiled=True)

    vmem = pl.BlockSpec(memory_space=pltpu.VMEM)
    smem = pl.BlockSpec(memory_space=pltpu.SMEM)
    anywhere = pl.BlockSpec(memory_space=pl.ANY)
    weights, b1 = pl.pallas_call(
        functools.partial(weights_kernel, tiles),
        out_shape=(
            jax.ShapeDtypeStruct((2, 9 * CH, CH), jnp.bfloat16),
            jax.ShapeDtypeStruct((3, 12 * CLAT, 2 * CH), jnp.bfloat16),
        ),
        in_specs=[
            smem,
            smem,
            anywhere,
            vmem,
        ],
        out_specs=(anywhere, vmem),
        scratch_shapes=[
            pltpu.VMEM((3, 3, 3, CH, CH), jnp.bfloat16),
            pltpu.VMEM((9, 2, CH, CH), jnp.bfloat16),
            pltpu.SemaphoreType.DMA((3,)),
            pltpu.SemaphoreType.DMA((18,)),
        ],
        compiler_params=pltpu.CompilerParams(vmem_limit_bytes=67_043_328),
        cost_estimate=pl.CostEstimate(flops=20_000_000, bytes_accessed=15_000_000, transcendentals=0),
    )(place, clip_index, middle_conv, first_conv)

    return pl.pallas_call(
        functools.partial(decode_kernel, slots),
        out_shape=jax.ShapeDtypeStruct((1, TF, 3, HL, WS * PATCH // 2), jnp.float32),
        in_specs=[smem, smem, vmem, vmem, vmem, anywhere, anywhere, vmem, vmem],
        out_specs=vmem,
        scratch_shapes=[
            pltpu.VMEM((4, 9 * CH, CH), jnp.bfloat16),
            pltpu.VMEM((4, 6 * CH, CH), jnp.bfloat16),
            pltpu.VMEM((LANE, CH), jnp.bfloat16),
            pltpu.VMEM((HL + 2 * PAD, TILES_WIN * LANE), jnp.float32),
            pltpu.VMEM((slots, CELLS, 192), jnp.bfloat16),
            pltpu.VMEM((4, COLS, LT, HL + 2 * PAD, LANE), jnp.float32),
            pltpu.VMEM((2, COLS, LT, HL, LANE), jnp.float32),
            pltpu.VMEM((16, CELLS, CH), jnp.bfloat16),
            pltpu.VMEM((2, 2, OUT_HALF, CH), jnp.float32),
            pltpu.SemaphoreType.DMA((36,)),
        ],
        compiler_params=pltpu.CompilerParams(vmem_limit_bytes=67_043_328),
    )(
        place,
        clip_index,
        came,
        b1,
        first_gain,
        weights,
        middle_conv,
        head_gain,
        head_weight.T,
    )


def solution(mesh):
    placed = (P(("group", "tile"), None, None), P("group"), P(), P(), P(), P(), P())
    return jax.shard_map(
        per_device,
        mesh=mesh,
        in_specs=placed,
        out_specs=P(("group", "tile"), None, None, None, None),
        check_vma=False,
    )
```

profile of v0, /device:TPU:0, one launch (start us, length us, event | category | flops | bytes accessed | tf_op | source)
XLA Modules:
  0.0 35.9 jit_solution(8480529509406202531)
XLA Ops:
  0.0 0.0 copy-start
  0.0 0.8 %copy-done = bf16[12,16,128]{2,1,0:T(8,128)(2,1)S(1)} copy-done((bf16[12,16,128]{2,1,0:T(8,128)(2,1)S(1)}, bf16[12,16,128]{2,1,0:T(8,128)(2,1)}, u32[]{:S(2)}) %copy-start) | copy-done | bytes 49176
  0.8 1.1 %shard_map.73 = bf16[16,36,128]{2,1,0:T(8,128)(2,1)} custom-call(bf16[12,16,128]{2,1,0:T(8,128)(2,1)S(1)} %copy-done), custom_call_target="tpu_custom_call" | custom-call | tf_op jit(solution)/shard_map/pallas_call | solution.py:318
  1.9 7.5 %all-to-all-start = ((bf16[16,36,128]{2,1,0:T(8,128)(2,1)}), bf16[16,36,128]{2,1,0:T(8,128)(2,1)}, u32[]{:S(2)}, u32[]{:S(2)}) async-start(bf16[16,36,128]{2,1,0:T(8,128)(2,1)} %shard_map.73), calls=%async_computation | async-start | bytes 327680 | tf_op jit(solution)/shard_map/all_to_all | solution.py:330
  9.4 7.9 %shard_map.74 = (bf16[2,3456,384]{2,1,0:T(8,128)(2,1)}, bf16[3,192,768]{2,1,0:T(8,128)(2,1)}) custom-call(s32[1]{0:T(128)} %bitcast.place_ref, s32[4]{0:T(128)} %clip_ref.3, bf16[3,3,3,384,384]{4,3,2,1,0:T(8,128)(2,1)} %mc_ref.3, bf16[3,3,3,16,384]{4,3,2,1,0:T(8,128)(2,1)} %fc_ref.1), custom_call_target="tpu_custom_call" | custom-call | flops 20000000 | bytes 15000000 | tf_op jit(solution)/shard_map/pallas_call | solution.py:335
  17.3 0.6 %all-to-all-done.recv_ref = bf16[16,36,128]{2,1,0:T(8,128)(2,1)} async-done(((bf16[16,36,128]{2,1,0:T(8,128)(2,1)}), bf16[16,36,128]{2,1,0:T(8,128)(2,1)}, u32[]{:S(2)}, u32[]{:S(2)}) %all-to-all-start) | async-done | bytes 147488 | tf_op jit(solution)/shard_map/all_to_all | solution.py:330
  17.9 17.8 %shard_map.75 = f32[1,2,3,48,128]{4,3,2,1,0:T(8,128)} custom-call(s32[1]{0:T(128)} %bitcast.place_ref, s32[4]{0:T(128)} %clip_ref.3, bf16[16,36,128]{2,1,0:T(8,128)(2,1)} %all-to-all-done.recv_ref, bf16[3,192,768]{2,1,0:T(8,128)(2,1)} %get-tuple-element.7.b1_ref, f32[384]{0:T(512)} %fg_ref.1, bf16[2,3456,384]{2,1,0:T(8,128)(2,1)} %get-tuple-element.8.wt_ref, ...), custom_call_target="tpu_custom_call" | custom-call | tf_op jit(solution)/shard_map/pallas_call | solution.py:358
Async XLA Ops:
  0.0 0.8 %copy-start = (bf16[12,16,128]{2,1,0:T(8,128)(2,1)S(1)}, bf16[12,16,128]{2,1,0:T(8,128)(2,1)}, u32[]{:S(2)}) copy-start(bf16[12,16,128]{2,1,0:T(8,128)(2,1)} %latents_ref.1) | copy-start | bytes 147460
  1.9 16.0 %all-to-all-start = ((bf16[16,36,128]{2,1,0:T(8,128)(2,1)}), bf16[16,36,128]{2,1,0:T(8,128)(2,1)}, u32[]{:S(2)}, u32[]{:S(2)}) async-start(bf16[16,36,128]{2,1,0:T(8,128)(2,1)} %shard_map.73), calls=%async_computation | async-start | bytes 327680 | tf_op jit(solution)/shard_map/all_to_all | solution.py:330
where the time goes:
time: 36.2 us; the launch traced here: 35.9 us
  Pallas kernels  26.9 us (74%)
  starting transfers between devices  7.46 us (21%)
  local copies, waits for them, and re-layouts  0.8 us (2%)
  waiting for transfers between devices  0.58 us (2%)
    pallas_call x1, Pallas kernels, per_device(): pl.pallas_call(functools.partial(decode_kernel, slots), out_shape=jax.Sha...  17.8 us
    pallas_call x1, Pallas kernels, per_device(): pl.pallas_call(functools.partial(weights_kernel, tiles), out_shape=(jax.S...  7.9 us
    all_to_all x1, starting transfers between devices, per_device(): came = lax.all_to_all(sent, 'tile', 0, 0, tiled=True)  7.46 us
    pallas_call x1, Pallas kernels, per_device(): pl.pallas_call(functools.partial(window_kernel, tiles), out_shape=jax.Sha...  1.13 us
    unnamed x2, local copies, waits for them, and re-layouts  0.8 us
  transfers between devices with their start and end apart: 1, of which 1 were waited for; matrix products, arithmetic and copies ran while one was open for 0% of the time, Pallas kernels for 22%

commit v1 on v0

--- a/solution.py
+++ b/solution.py
@@ -179,9 +179,7 @@
             total = part if total is None else total + part
         for side in range(2):
             x = total[:, side * CH : (side + 1) * CH]
-            a = silu_of_twice(x * inv_rms(x) * gain)
-            if keeps[t] is not None:
-                a = a * keeps[t]
+            a = silu_of_twice(x * inv_rms(x) * (gain if keeps[t] is None else gain * keeps[t]))
             for pair in range(PAIRS):
                 cut = slice(pair * HL, (pair + 1) * HL)
                 piece = a[cut]
@@ -215,7 +213,7 @@
                 xa[k, pl.ds(at, HL), lt * LANE : (lt + 1) * LANE] = both
         return carry
 
-    lax.fori_loop(0, PAIRS, transform, 0, unroll=2)
+    lax.fori_loop(0, PAIRS, transform, 0, unroll=5)
 
     deep = 3 * CH
     for m in range(4):

time: 36.2 us -> 36 us (level)
  no operation moved by 1% of the time
where the time goes in v1:
time: 36 us; the launch traced here: 35.7 us
  Pallas kernels  26.7 us (74%)
  starting transfers between devices  7.46 us (21%)
  local copies, waits for them, and re-layouts  0.8 us (2%)
  waiting for transfers between devices  0.58 us (2%)
    pallas_call x1, Pallas kernels, per_device(): pl.pallas_call(functools.partial(decode_kernel, slots), out_shape=jax.Sha...  17.7 us
    pallas_call x1, Pallas kernels, per_device(): pl.pallas_call(functools.partial(weights_kernel, tiles), out_shape=(jax.S...  7.9 us
    all_to_all x1, starting transfers between devices, per_device(): came = lax.all_to_all(sent, 'tile', 0, 0, tiled=True)  7.46 us
    pallas_call x1, Pallas kernels, per_device(): pl.pallas_call(functools.partial(window_kernel, tiles), out_shape=jax.Sha...  1.13 us
    unnamed x2, local copies, waits for them, and re-layouts  0.8 us
  transfers between devices with their start and end apart: 1, of which 1 were waited for; matrix products, arithmetic and copies ran while one was open for 0% of the time, Pallas kernels for 22%

profile of v1, /device:TPU:0, one launch (start us, length us, event | category | flops | bytes accessed | tf_op | source)
XLA Modules:
  0.0 35.7 jit_solution(11599098049064408849)
XLA Ops:
  0.0 0.0 copy-start
  0.0 0.8 %copy-done = bf16[12,16,128]{2,1,0:T(8,128)(2,1)S(1)} copy-done((bf16[12,16,128]{2,1,0:T(8,128)(2,1)S(1)}, bf16[12,16,128]{2,1,0:T(8,128)(2,1)}, u32[]{:S(2)}) %copy-start) | copy-done | bytes 49176
  0.8 1.1 %shard_map.73 = bf16[16,36,128]{2,1,0:T(8,128)(2,1)} custom-call(bf16[12,16,128]{2,1,0:T(8,128)(2,1)S(1)} %copy-done), custom_call_target="tpu_custom_call" | custom-call | tf_op jit(solution)/shard_map/pallas_call | solution.py:316
  1.9 7.5 %all-to-all-start = ((bf16[16,36,128]{2,1,0:T(8,128)(2,1)}), bf16[16,36,128]{2,1,0:T(8,128)(2,1)}, u32[]{:S(2)}, u32[]{:S(2)}) async-start(bf16[16,36,128]{2,1,0:T(8,128)(2,1)} %shard_map.73), calls=%async_computation | async-start | bytes 327680 | tf_op jit(solution)/shard_map/all_to_all | solution.py:328
  9.4 7.9 %shard_map.74 = (bf16[2,3456,384]{2,1,0:T(8,128)(2,1)}, bf16[3,192,768]{2,1,0:T(8,128)(2,1)}) custom-call(s32[1]{0:T(128)} %bitcast.place_ref, s32[4]{0:T(128)} %clip_ref.3, bf16[3,3,3,384,384]{4,3,2,1,0:T(8,128)(2,1)} %mc_ref.3, bf16[3,3,3,16,384]{4,3,2,1,0:T(8,128)(2,1)} %fc_ref.1), custom_call_target="tpu_custom_call" | custom-call | flops 20000000 | bytes 15000000 | tf_op jit(solution)/shard_map/pallas_call | solution.py:333
  17.3 0.6 %all-to-all-done.recv_ref = bf16[16,36,128]{2,1,0:T(8,128)(2,1)} async-done(((bf16[16,36,128]{2,1,0:T(8,128)(2,1)}), bf16[16,36,128]{2,1,0:T(8,128)(2,1)}, u32[]{:S(2)}, u32[]{:S(2)}) %all-to-all-start) | async-done | bytes 147488 | tf_op jit(solution)/shard_map/all_to_all | solution.py:328
  17.9 17.7 %shard_map.75 = f32[1,2,3,48,128]{4,3,2,1,0:T(8,128)} custom-call(s32[1]{0:T(128)} %bitcast.place_ref, s32[4]{0:T(128)} %clip_ref.3, bf16[16,36,128]{2,1,0:T(8,128)(2,1)} %all-to-all-done.recv_ref, bf16[3,192,768]{2,1,0:T(8,128)(2,1)} %get-tuple-element.7.b1_ref, f32[384]{0:T(512)} %fg_ref.1, bf16[2,3456,384]{2,1,0:T(8,128)(2,1)} %get-tuple-element.8.wt_ref, ...), custom_call_target="tpu_custom_call" | custom-call | tf_op jit(solution)/shard_map/pallas_call | solution.py:356
Async XLA Ops:
  0.0 0.8 %copy-start = (bf16[12,16,128]{2,1,0:T(8,128)(2,1)S(1)}, bf16[12,16,128]{2,1,0:T(8,128)(2,1)}, u32[]{:S(2)}) copy-start(bf16[12,16,128]{2,1,0:T(8,128)(2,1)} %latents_ref.1) | copy-start | bytes 147460
  1.9 16.0 %all-to-all-start = ((bf16[16,36,128]{2,1,0:T(8,128)(2,1)}), bf16[16,36,128]{2,1,0:T(8,128)(2,1)}, u32[]{:S(2)}, u32[]{:S(2)}) async-start(bf16[16,36,128]{2,1,0:T(8,128)(2,1)} %shard_map.73), calls=%async_computation | async-start | bytes 327680 | tf_op jit(solution)/shard_map/all_to_all | solution.py:328
